TPU v7x, 32 devices: a whole 2x2x4 slice. The times are simulated.
32 devices in a mesh: fsdp: 2 (over core), ctx: 4 (over y, x), tensor: 4 (over z).
Axes of the slice: x: 2, y: 2, z: 4, core: 2. Of those that a mesh axis runs over, the one named last changes fastest.
Arguments:
- tokens: bfloat16 [4, 1024, 2048], P('fsdp', ('ctx', 'tensor')), may hold values from -6 to 6
- segments: int32 [4, 1024], P('fsdp'), may hold values from 0 to 6, as said below
- positions: int32 [4, 1024], P('fsdp'), may hold values from 0 to 1226, as said below
- query_weight: bfloat16 [2048, 2048], P(('fsdp', 'ctx'), 'tensor'), may hold values from -0.125 to 0.125
- key_weight: bfloat16 [2048, 2048], P(('fsdp', 'ctx'), 'tensor'), may hold values from -0.125 to 0.125
- value_weight: bfloat16 [2048, 2048], P(('fsdp', 'ctx'), 'tensor'), may hold values from -0.125 to 0.125
- output_weight: bfloat16 [2048, 2048], P(('fsdp', 'ctx'), 'tensor'), may hold values from -0.125 to 0.125
- gate_weight: bfloat16 [2048, 8192], P(('fsdp', 'ctx'), 'tensor'), may hold values from -0.125 to 0.125
- up_projection_weight: bfloat16 [2048, 8192], P(('fsdp', 'ctx'), 'tensor'), may hold values from -0.125 to 0.125
- down_weight: bfloat16 [2048, 8192], P(('fsdp', 'ctx'), 'tensor'), may hold values from -0.0625 to 0.0625
- query_gain: float32 [2048], replicated, may hold values from 0.5 to 1.5
- key_gain: float32 [2048], replicated, may hold values from 0.5 to 1.5
- attention_gain: float32 [2048], replicated, may hold values from 0.5 to 1.5
- feedforward_gain: float32 [2048], replicated, may hold values from 0.5 to 1.5
- cotangent: bfloat16 [4, 1024, 2048], P('fsdp', ('ctx', 'tensor')), may hold values from -6 to 6
Outputs:
- block_out: bfloat16 [4, 1024, 2048], P('fsdp', ('ctx', 'tensor'))
- input_grad: float32 [4, 1024, 2048], P('fsdp', ('ctx', 'tensor'))
- query_weight_grad: float32 [2048, 2048], P(('fsdp', 'ctx'), 'tensor')
- key_weight_grad: float32 [2048, 2048], P(('fsdp', 'ctx'), 'tensor')
- value_weight_grad: float32 [2048, 2048], P(('fsdp', 'ctx'), 'tensor')
- output_weight_grad: float32 [2048, 2048], P(('fsdp', 'ctx'), 'tensor')
- gate_weight_grad: float32 [2048, 8192], P(('fsdp', 'ctx'), 'tensor')
- up_weight_grad: float32 [2048, 8192], P(('fsdp', 'ctx'), 'tensor')
- down_weight_grad: float32 [2048, 8192], P(('fsdp', 'ctx'), 'tensor')
- query_gain_grad: float32 [2048], replicated
- key_gain_grad: float32 [2048], replicated
- attention_gain_grad: float32 [2048], replicated
- feedforward_gain_grad: float32 [2048], replicated
Inputs may be any that keep to these rules, and one draw needn't show every extreme that they name: `segments`: in each sequence the numbers start at 0 and rise by one where a new document begins; documents hold a fifth of 1024 (rounded down) to 2047 tokens, and the first may have begun before the sequence. `positions`: each token's index in its document; it rises by one from token to token within a document and is 0 where a document begins inside the sequence.
All inputs are finite; a program needn't handle non-finite values.
Results may differ from a plain program's by a relative error of at most 0.017.
Values may be sent and summed in bfloat16 or wider, within the bound.
A program may use at most 256 MiB of HBM per device.

v0:
```python
import jax
import jax.numpy as jnp
from jax import lax
from jax.sharding import PartitionSpec as P

D = 2048
HD = 128
epsilon = 1e-06
rope_theta = 500000.0
masked_score = -1e30


def rope_tables(position_ids):
    freq_index = jnp.arange(HD // 2, dtype=jnp.float32)
    inverse = rope_theta ** (-2.0 * freq_index / HD)
    angles = position_ids.astype(jnp.float32)[..., None] * inverse
    return (jnp.cos(angles), jnp.sin(angles))


def rotate(values, cosine, sine):
    half = values.shape[-1] // 2
    first_half = values[..., :half]
    second_half = values[..., half:]
    cos_wide = cosine[..., None, :]
    sin_wide = sine[..., None, :]
    return jnp.concatenate(
        [
            first_half * cos_wide - second_half * sin_wide,
            second_half * cos_wide + first_half * sin_wide,
        ],
        axis=-1,
    )


def unrotate(values, cosine, sine):
    half = values.shape[-1] // 2
    first_half = values[..., :half]
    second_half = values[..., half:]
    cos_wide = cosine[..., None, :]
    sin_wide = sine[..., None, :]
    return jnp.concatenate(
        [
            first_half * cos_wide + second_half * sin_wide,
            second_half * cos_wide - first_half * sin_wide,
        ],
        axis=-1,
    )


def root_mean_square_scale(values):
    return lax.rsqrt(jnp.mean(values * values, axis=-1, keepdims=True) + epsilon)


def norm_back(grad_unit, unit, scale):
    return scale * (grad_unit - unit * jnp.mean(grad_unit * unit, axis=-1, keepdims=True))


def project(matrix_rows, weight_matrix):
    return jnp.einsum("xmj,je->xme", matrix_rows, weight_matrix, preferred_element_type=jnp.float32)


def project_back(matrix_rows, weight_matrix):
    return jnp.einsum("rhy,iy->rhi", matrix_rows, weight_matrix, preferred_element_type=jnp.float32)


def weight_term(left_operand_rows, right_operand_rows):
    return jnp.einsum(
        "prt,pre->te", left_operand_rows, right_operand_rows, preferred_element_type=jnp.float32
    )


def gather_tokens(matrix_rows):
    return lax.all_gather(matrix_rows, "tensor", axis=1, tiled=True)


def sum_tokens(terms):
    return lax.psum_scatter(terms, "tensor", scatter_dimension=1, tiled=True)


def body(
    tokens,
    segments,
    positions,
    query_weight,
    key_weight,
    value_weight,
    output_weight,
    gate_weight,
    up_projection_weight,
    down_weight,
    query_gain,
    key_gain,
    attention_gain,
    feedforward_gain,
    cotangent,
):
    ctx_index = lax.axis_index("ctx")
    tensor_index = lax.axis_index("tensor")
    gathered = (
        lax.all_gather(query_weight, ("fsdp", "ctx"), axis=0, tiled=True),
        lax.all_gather(key_weight, ("fsdp", "ctx"), axis=0, tiled=True),
        lax.all_gather(value_weight, ("fsdp", "ctx"), axis=0, tiled=True),
        lax.all_gather(output_weight, ("fsdp", "ctx"), axis=0, tiled=True),
        lax.all_gather(gate_weight, ("fsdp", "ctx"), axis=0, tiled=True),
        lax.all_gather(up_projection_weight, ("fsdp", "ctx"), axis=0, tiled=True),
        lax.all_gather(down_weight, ("fsdp", "ctx"), axis=0, tiled=True),
    )
    query_full, key_full, value_full, output_full, gate_full, up_full, down_full = gathered
    width_local = query_full.shape[1]
    heads_local = width_local // HD
    gain_start = tensor_index * width_local
    query_gain_local = lax.dynamic_slice_in_dim(query_gain, gain_start, width_local)
    key_gain_local = lax.dynamic_slice_in_dim(key_gain, gain_start, width_local)
    score_scale = HD ** (-0.5)
    tokens_block = gather_tokens(tokens)
    seq_count = tokens_block.shape[0]
    block_len = tokens_block.shape[1]
    full_len = segments.shape[1]
    query_lin = project(tokens_block, query_full)
    key_lin = project(tokens_block, key_full)
    value_lin = project(tokens_block, value_full)
    query_squared, key_sq = lax.psum(
        (jnp.sum(query_lin * query_lin, axis=-1), jnp.sum(key_lin * key_lin, axis=-1)), "tensor"
    )
    query_scale = lax.rsqrt(query_squared / D + epsilon)[..., None]
    key_scale = lax.rsqrt(key_sq / D + epsilon)[..., None]
    query_unit = query_lin * query_scale
    key_unit = key_lin * key_scale
    block_pos = lax.dynamic_slice_in_dim(positions, ctx_index * block_len, block_len, 1)
    cosine, sine = rope_tables(block_pos)

    def heads_of(values):
        return values.reshape(seq_count, block_len, heads_local, HD)

    query_rot = rotate(heads_of(query_unit * query_gain_local), cosine, sine).astype(jnp.bfloat16)
    key_rot = rotate(heads_of(key_unit * key_gain_local), cosine, sine).astype(jnp.bfloat16)
    value_rot = heads_of(value_lin).astype(jnp.bfloat16)
    query_heads, key_heads, value_heads = (
        lax.all_to_all(query_rot, "ctx", split_axis=2, concat_axis=1, tiled=True),
        lax.all_to_all(key_rot, "ctx", split_axis=2, concat_axis=1, tiled=True),
        lax.all_to_all(value_rot, "ctx", split_axis=2, concat_axis=1, tiled=True),
    )
    token_index = jnp.arange(full_len, dtype=jnp.int32)
    allowed = (segments[:, :, None] == segments[:, None, :]) & (
        token_index[None, :, None] >= token_index[None, None, :]
    )
    allowed = allowed[:, None]

    def masked_scores():
        raw_scores = (
            jnp.einsum(
                "sqhd,skhd->shqk", query_heads, key_heads, preferred_element_type=jnp.float32
            )
            * score_scale
        )
        return jnp.where(allowed, raw_scores, masked_score)

    scores = masked_scores()
    top_score = jnp.max(scores, axis=-1, keepdims=True)
    log_total = top_score + jnp.log(jnp.sum(jnp.exp(scores - top_score), axis=-1, keepdims=True))
    probs_b = jnp.exp(scores - log_total).astype(jnp.bfloat16)
    attended = jnp.einsum(
        "shqk,skhd->sqhd", probs_b, value_heads, preferred_element_type=jnp.float32
    ).astype(jnp.bfloat16)
    attended_block = lax.all_to_all(
        attended, "ctx", split_axis=1, concat_axis=2, tiled=True
    ).reshape(seq_count, block_len, width_local)
    attention_out = sum_tokens(project_back(attended_block, output_full))
    attention_scale = root_mean_square_scale(attention_out)
    attention_unit = attention_out * attention_scale
    hidden_state = tokens.astype(jnp.float32) + attention_unit * attention_gain
    hidden_block = gather_tokens(hidden_state.astype(jnp.bfloat16))
    gate_lin = project(hidden_block, gate_full)
    up_lin = project(hidden_block, up_full)
    gate_sig = jax.nn.sigmoid(gate_lin)
    gate_act = gate_lin * gate_sig
    mixed = (gate_act * up_lin).astype(jnp.bfloat16)
    mixed_out = sum_tokens(project_back(mixed, down_full))
    mixed_scale = root_mean_square_scale(mixed_out)
    mixed_unit = mixed_out * mixed_scale
    block_out = (hidden_state + mixed_unit * feedforward_gain).astype(jnp.bfloat16)
    back_weights = (
        lax.all_gather(query_weight, ("fsdp", "ctx"), axis=0, tiled=True),
        lax.all_gather(key_weight, ("fsdp", "ctx"), axis=0, tiled=True),
        lax.all_gather(value_weight, ("fsdp", "ctx"), axis=0, tiled=True),
        lax.all_gather(output_weight, ("fsdp", "ctx"), axis=0, tiled=True),
        lax.all_gather(gate_weight, ("fsdp", "ctx"), axis=0, tiled=True),
        lax.all_gather(up_projection_weight, ("fsdp", "ctx"), axis=0, tiled=True),
        lax.all_gather(down_weight, ("fsdp", "ctx"), axis=0, tiled=True),
    )
    query_back, key_back, value_back, output_back, gate_back, up_back, down_back = back_weights
    upstream = cotangent.astype(jnp.float32)
    ffn_gain_grad = jnp.sum(upstream * mixed_unit, axis=(0, 1))
    mixed_grad = norm_back(upstream * feedforward_gain, mixed_unit, mixed_scale).astype(
        jnp.bfloat16
    )
    mixed_grad_block = gather_tokens(mixed_grad)
    inner_grad = project(mixed_grad_block, down_back)
    down_wgrad = weight_term(mixed_grad_block, mixed)
    gate_lin_grad = (inner_grad * up_lin * gate_sig * (1.0 + gate_lin * (1.0 - gate_sig))).astype(
        jnp.bfloat16
    )
    up_lin_grad = (inner_grad * gate_act).astype(jnp.bfloat16)
    gate_wgrad = weight_term(hidden_block, gate_lin_grad)
    up_wgrad = weight_term(hidden_block, up_lin_grad)
    hidden_grad = upstream + sum_tokens(
        project_back(gate_lin_grad, gate_back) + project_back(up_lin_grad, up_back)
    )
    attn_gain_grad = jnp.sum(hidden_grad * attention_unit, axis=(0, 1))
    attention_grad = norm_back(
        hidden_grad * attention_gain, attention_unit, attention_scale
    ).astype(jnp.bfloat16)
    attention_grad_block = gather_tokens(attention_grad)
    attended_output_gradient = project(attention_grad_block, output_back).astype(jnp.bfloat16)
    output_wgrad = weight_term(attention_grad_block, attended_block)
    attended_grad_heads = lax.all_to_all(
        heads_of(attended_output_gradient), "ctx", split_axis=2, concat_axis=1, tiled=True
    )
    probs_full = jnp.exp(masked_scores() - log_total)
    probs_again = probs_full.astype(jnp.bfloat16)
    value_grad_heads = jnp.einsum(
        "shqk,sqhd->skhd", probs_again, attended_grad_heads, preferred_element_type=jnp.float32
    ).astype(jnp.bfloat16)
    prob_grad = jnp.einsum(
        "sqhd,skhd->shqk", attended_grad_heads, value_heads, preferred_element_type=jnp.float32
    )
    delta_rows = jnp.einsum(
        "sqhd,sqhd->shq", attended_grad_heads, attended, preferred_element_type=jnp.float32
    )
    score_grad = (probs_full * (prob_grad - delta_rows[..., None])).astype(jnp.bfloat16)
    query_grad_heads = (
        jnp.einsum("shqk,skhd->sqhd", score_grad, key_heads, preferred_element_type=jnp.float32)
        * score_scale
    ).astype(jnp.bfloat16)
    key_grad_heads = (
        jnp.einsum("shqk,sqhd->skhd", score_grad, query_heads, preferred_element_type=jnp.float32)
        * score_scale
    ).astype(jnp.bfloat16)
    query_grad_rot, key_grad_rot, value_grad_rot = (
        lax.all_to_all(query_grad_heads, "ctx", split_axis=1, concat_axis=2, tiled=True),
        lax.all_to_all(key_grad_heads, "ctx", split_axis=1, concat_axis=2, tiled=True),
        lax.all_to_all(value_grad_heads, "ctx", split_axis=1, concat_axis=2, tiled=True),
    )
    query_grad_n = unrotate(query_grad_rot.astype(jnp.float32), cosine, sine).reshape(
        seq_count, block_len, width_local
    )
    key_grad_n = unrotate(key_grad_rot.astype(jnp.float32), cosine, sine).reshape(
        seq_count, block_len, width_local
    )
    query_gain_part = jnp.sum(query_grad_n * query_unit, axis=(0, 1))
    key_gain_part = jnp.sum(key_grad_n * key_unit, axis=(0, 1))
    query_grad_u = query_grad_n * query_gain_local
    key_grad_u = key_grad_n * key_gain_local
    query_inner, key_inner = lax.psum(
        (jnp.sum(query_grad_u * query_unit, axis=-1), jnp.sum(key_grad_u * key_unit, axis=-1)),
        "tensor",
    )
    query_pre = (query_scale * (query_grad_u - query_unit * (query_inner / D)[..., None])).astype(
        jnp.bfloat16
    )
    key_pre = (key_scale * (key_grad_u - key_unit * (key_inner / D)[..., None])).astype(
        jnp.bfloat16
    )
    value_pre = value_grad_rot.reshape(seq_count, block_len, width_local)
    input_attn = sum_tokens(
        project_back(query_pre, query_back)
        + project_back(key_pre, key_back)
        + project_back(value_pre, value_back)
    )
    input_grad = hidden_grad + input_attn
    query_wgrad = weight_term(tokens_block, query_pre)
    key_wgrad = weight_term(tokens_block, key_pre)
    value_wgrad = weight_term(tokens_block, value_pre)
    query_gain_full = lax.dynamic_update_slice_in_dim(
        jnp.zeros((D,), jnp.float32), query_gain_part, gain_start, 0
    )
    key_gain_full = lax.dynamic_update_slice_in_dim(
        jnp.zeros((D,), jnp.float32), key_gain_part, gain_start, 0
    )
    query_gain_grad, key_gain_grad, attention_gain_grad, feedforward_gain_grad = lax.psum(
        (query_gain_full, key_gain_full, attn_gain_grad, ffn_gain_grad), ("fsdp", "ctx", "tensor")
    )
    (
        query_reduced,
        key_reduced,
        value_reduced,
        output_reduced,
        gate_reduced,
        up_reduced,
        down_reduced,
    ) = (
        lax.psum_scatter(query_wgrad, ("fsdp", "ctx"), scatter_dimension=0, tiled=True),
        lax.psum_scatter(key_wgrad, ("fsdp", "ctx"), scatter_dimension=0, tiled=True),
        lax.psum_scatter(value_wgrad, ("fsdp", "ctx"), scatter_dimension=0, tiled=True),
        lax.psum_scatter(output_wgrad, ("fsdp", "ctx"), scatter_dimension=0, tiled=True),
        lax.psum_scatter(gate_wgrad, ("fsdp", "ctx"), scatter_dimension=0, tiled=True),
        lax.psum_scatter(up_wgrad, ("fsdp", "ctx"), scatter_dimension=0, tiled=True),
        lax.psum_scatter(down_wgrad, ("fsdp", "ctx"), scatter_dimension=0, tiled=True),
    )
    return (
        block_out,
        input_grad,
        query_reduced,
        key_reduced,
        value_reduced,
        output_reduced,
        gate_reduced,
        up_reduced,
        down_reduced,
        query_gain_grad,
        key_gain_grad,
        attention_gain_grad,
        feedforward_gain_grad,
    )


def solution(mesh):
    in_specs = (
        P("fsdp", ("ctx", "tensor"), None),
        P("fsdp", None),
        P("fsdp", None),
        P(("fsdp", "ctx"), "tensor"),
        P(("fsdp", "ctx"), "tensor"),
        P(("fsdp", "ctx"), "tensor"),
        P(("fsdp", "ctx"), "tensor"),
        P(("fsdp", "ctx"), "tensor"),
        P(("fsdp", "ctx"), "tensor"),
        P(("fsdp", "ctx"), "tensor"),
        P(),
        P(),
        P(),
        P(),
        P("fsdp", ("ctx", "tensor"), None),
    )
    out_specs = (
        P("fsdp", ("ctx", "tensor"), None),
        P("fsdp", ("ctx", "tensor"), None),
        P(("fsdp", "ctx"), "tensor"),
        P(("fsdp", "ctx"), "tensor"),
        P(("fsdp", "ctx"), "tensor"),
        P(("fsdp", "ctx"), "tensor"),
        P(("fsdp", "ctx"), "tensor"),
        P(("fsdp", "ctx"), "tensor"),
        P(("fsdp", "ctx"), "tensor"),
        P(),
        P(),
        P(),
        P(),
    )
    return jax.shard_map(body, mesh=mesh, in_specs=in_specs, out_specs=out_specs, check_vma=False)
```

profile of v0, /device:TPU:0, one launch (start us, length us, event | category | flops | bytes accessed | tf_op | source)
XLA Modules:
  0.0 1508.3 jit_solution(17496973479163622820)
XLA Ops:
  14.5 43.4 %all-gather.12.cloned.1.call-done = bf16[2,256,2048]{2,1,0:T(8,128)(2,1)} async-done(((bf16[2,64,2048]{2,1,0:T(8,128)(2,1)}), bf16[2,256,2048]{2,1,0:T(8,128)(2,1)}) %all-gather.12.cloned.1.call-update) | async-done | bytes 2097168 | tf_op jit(solution)/shard_map/all_gather | solution.py:73
  58.0 28.5 %all-gather.16.cloned.1.call-done = bf16[2048,512]{1,0:T(8,128)(2,1)} async-done(((bf16[256,512]{1,0:T(8,128)(2,1)}), bf16[2048,512]{1,0:T(8,128)(2,1)}) %all-gather.16.cloned.1.call-update) | async-done | bytes 2097168 | tf_op jit(solution)/shard_map/all_gather | solution.py:100
  86.5 3.5 multiply_reduce_fusion.8
  90.0 26.1 %all-gather.18.cloned.1.call-done = bf16[2048,512]{1,0:T(8,128)(2,1)} async-done(((bf16[256,512]{1,0:T(8,128)(2,1)}), bf16[2048,512]{1,0:T(8,128)(2,1)}) %all-gather.18.cloned.1.call-update) | async-done | bytes 2097168 | tf_op jit(solution)/shard_map/all_gather | solution.py:101
  116.2 3.8 multiply_reduce_fusion.7
  120.0 11.7 all-reduce.2
  132.8 2.5 reshape.204
  135.3 3.9 fusion.62
  146.0 3.5 all-to-all-start.2
  151.6 4.4 all-to-all-done.2
  156.0 3.5 all-to-all-start.1
  159.5 2.8 fusion.47
  163.3 2.8 all-to-all-done.1
  166.1 4.1 all-to-all-start
  174.0 7.8 all-to-all-done
  185.3 4.0 fusion.63
  195.3 10.6 all_to_all.108
  209.1 4.8 fusion.19
  214.8 75.6 %reduce-scatter.12.cloned.1.call-done = f32[2,64,2048]{2,1,0:T(8,128)} async-done(((f32[2,256,2048]{2,1,0:T(8,128)}), f32[2,64,2048]{2,1,0:T(8,128)}) %reduce-scatter.12.cloned.1.call-update) | async-done | bytes 1048592 | tf_op jit(solution)/shard_map/reduce_scatter | solution.py:77
  295.9 51.1 %all-gather.24.cloned.1.call-done = bf16[2048,2048]{1,0:T(8,128)(2,1)} async-done(((bf16[256,2048]{1,0:T(8,128)(2,1)}), bf16[2048,2048]{1,0:T(8,128)(2,1)}) %all-gather.24.cloned.1.call-update) | async-done | bytes 8388624 | tf_op jit(solution)/shard_map/all_gather | solution.py:104
  347.0 47.8 %all-gather.22.cloned.1.call-done = bf16[2,256,2048]{2,1,0:T(8,128)(2,1)} async-done(((bf16[2,64,2048]{2,1,0:T(8,128)(2,1)}), bf16[2,256,2048]{2,1,0:T(8,128)(2,1)}) %all-gather.22.cloned.1.call-update) | async-done | bytes 2097168 | tf_op jit(solution)/shard_map/all_gather | solution.py:73
  394.8 10.6 fusion.10
  405.4 44.4 %all-gather.26.cloned.1.call-done = bf16[2048,2048]{1,0:T(8,128)(2,1)} async-done(((bf16[256,2048]{1,0:T(8,128)(2,1)}), bf16[2048,2048]{1,0:T(8,128)(2,1)}) %all-gather.26.cloned.1.call-update) | async-done | bytes 8388624 | tf_op jit(solution)/shard_map/all_gather | solution.py:105
  449.8 12.5 multiply_convert_fusion.3
  462.3 43.5 %all-gather.28.cloned.1.call-done = bf16[2048,2048]{1,0:T(8,128)(2,1)} async-done(((bf16[256,2048]{1,0:T(8,128)(2,1)}), bf16[2048,2048]{1,0:T(8,128)(2,1)}) %all-gather.28.cloned.1.call-update) | async-done | bytes 8388624 | tf_op jit(solution)/shard_map/all_gather | solution.py:106
  505.8 10.5 fusion.2
  516.5 76.9 %reduce-scatter.14.cloned.1.call-done = f32[2,64,2048]{2,1,0:T(8,128)} async-done(((f32[2,256,2048]{2,1,0:T(8,128)}), f32[2,64,2048]{2,1,0:T(8,128)}) %reduce-scatter.14.cloned.1.call-update) | async-done | bytes 1048592 | tf_op jit(solution)/shard_map/reduce_scatter | solution.py:77
  596.4 2.3 fusion.55
  598.9 46.1 %all-gather.30.cloned.1.call-done = bf16[2,256,2048]{2,1,0:T(8,128)(2,1)} async-done(((bf16[2,64,2048]{2,1,0:T(8,128)(2,1)}), bf16[2,256,2048]{2,1,0:T(8,128)(2,1)}) %all-gather.30.cloned.1.call-update) | async-done | bytes 2097168 | tf_op jit(solution)/shard_map/all_gather | solution.py:73
  645.0 11.9 multiply_convert_fusion.2
  656.9 8.5 fusion.4
  665.4 9.5 fusion.14
  675.0 75.7 %reduce-scatter.16.cloned.1.call-done = f32[2,64,2048]{2,1,0:T(8,128)} async-done(((f32[2,256,2048]{2,1,0:T(8,128)}), f32[2,64,2048]{2,1,0:T(8,128)}) %reduce-scatter.16.cloned.1.call-update) | async-done | bytes 1048592 | tf_op jit(solution)/shard_map/reduce_scatter | solution.py:77
  752.8 3.3 multiply_convert_fusion.6
  756.2 46.3 %all-gather.32.cloned.1.call-done = bf16[2,256,2048]{2,1,0:T(8,128)(2,1)} async-done(((bf16[2,64,2048]{2,1,0:T(8,128)(2,1)}), bf16[2,256,2048]{2,1,0:T(8,128)(2,1)}) %all-gather.32.cloned.1.call-update) | async-done | bytes 2097168 | tf_op jit(solution)/shard_map/all_gather | solution.py:73
  802.4 3.5 fusion.44
  806.0 11.8 all_to_all.109
  817.9 5.7 fusion.50
  824.9 9.8 all_to_all.110
  837.9 3.3 convolution_bitcast_fusion.4
  843.9 6.0 multiply_convert_fusion
  853.8 4.1 all-to-all-start.5
  857.9 3.7 fusion.42
  862.7 4.1 all-to-all-done.5
  866.9 4.2 all-to-all-start.6
  872.2 9.2 all-to-all-done.6
  886.2 10.2 all-reduce.1
  896.3 2.4 multiply_convert_fusion.4
  899.5 3.3 convolution_bitcast_fusion.5
  905.7 3.3 convolution_bitcast_fusion.6
  909.5 3.2 fusion.21
  914.6 3.4 add_add_fusion
  919.0 4.9 convolution_bitcast_fusion.3
  923.9 12.6 convolution_bitcast_fusion
  938.1 9.8 convolution_bitcast_fusion.2
  948.2 9.8 convolution_bitcast_fusion.1
  958.5 39.2 %all-reduce = (f32[2048]{0:T(1024)}, f32[2048]{0:T(1024)}, f32[2048]{0:T(1024)}, f32[2048]{0:T(1024)}) all-reduce(f32[2048]{0:T(1024)S(1)} %dynamic_update_slice.6, f32[2048]{0:T(1024)S(1)} %dynamic_update_slice.7, f32[2048]{0:T(1024)S(1)} %get-tuple-element.52, ...), channel_id=1, replica_groups=mesh['fsdp'=2,'ctx'=4,'tensor'=4] {'fsdp','ctx','tensor'}, use_global_device_ids=true, to_apply=%region_26.27 | all-reduce | flops 8192 | bytes 65536 | tf_op jit(solution)/shard_map/psum | solution.py:280
  1001.8 3.9 reduce-scatter.20.cloned.1.call-done
  1007.8 76.9 %reduce-scatter.18.cloned.1.call-done = f32[2,64,2048]{2,1,0:T(8,128)} async-done(((f32[2,256,2048]{2,1,0:T(8,128)}), f32[2,64,2048]{2,1,0:T(8,128)}) %reduce-scatter.18.cloned.1.call-update) | async-done | bytes 1048592 | tf_op jit(solution)/shard_map/reduce_scatter | solution.py:77
  1084.7 2.4 fusion.60
  1087.1 53.2 %reduce-scatter.26.cloned.1.call-done = f32[256,512]{1,0:T(8,128)} async-done(((f32[2048,512]{1,0:T(8,128)}), f32[256,512]{1,0:T(8,128)}) %reduce-scatter.26.cloned.1.call-update) | async-done | bytes 524304 | tf_op jit(solution)/shard_map/reduce_scatter | solution.py:295
  1140.3 120.2 %reduce-scatter.32.cloned.1.call-done = f32[256,2048]{1,0:T(8,128)} async-done(((f32[2048,2048]{1,0:T(8,128)}), f32[256,2048]{1,0:T(8,128)}) %reduce-scatter.32.cloned.1.call-update) | async-done | bytes 2097168 | tf_op jit(solution)/shard_map/reduce_scatter | solution.py:298
  1260.5 120.4 %reduce-scatter.28.cloned.1.call-done = f32[256,2048]{1,0:T(8,128)} async-done(((f32[2048,2048]{1,0:T(8,128)}), f32[256,2048]{1,0:T(8,128)}) %reduce-scatter.28.cloned.1.call-update) | async-done | bytes 2097168 | tf_op jit(solution)/shard_map/reduce_scatter | solution.py:296
  1380.9 120.4 %reduce-scatter.30.cloned.1.call-done = f32[256,2048]{1,0:T(8,128)} async-done(((f32[2048,2048]{1,0:T(8,128)}), f32[256,2048]{1,0:T(8,128)}) %reduce-scatter.30.cloned.1.call-update) | async-done | bytes 2097168 | tf_op jit(solution)/shard_map/reduce_scatter | solution.py:297
  (194 shorter events, 80.1 us)
Async XLA Ops:
  7.2 50.8 %all-gather.12.cloned.1.call-start = ((), (), s32[]{:S(2)}) async-start(), calls=%async_computation.19 | async-start | bytes 2621440 | tf_op jit(solution)/shard_map/all_gather | solution.py:73
  7.9 78.6 %all-gather.16.cloned.1.call-start = ((), (), s32[]{:S(2)}) async-start(), calls=%async_computation.21 | async-start | bytes 2359296 | tf_op jit(solution)/shard_map/all_gather | solution.py:100
  8.7 107.5 %all-gather.18.cloned.1.call-start = ((), (), s32[]{:S(2)}) async-start(), calls=%async_computation.22 | async-start | bytes 2359296 | tf_op jit(solution)/shard_map/all_gather | solution.py:101
  9.4 150.1 %all-gather.14.cloned.1.call-start = ((), (), s32[]{:S(2)}) async-start(), calls=%async_computation.20 | async-start | bytes 2359296 | tf_op jit(solution)/shard_map/all_gather | solution.py:102
  10.0 198.3 %all-gather.20.cloned.1.call-start = ((), (), s32[]{:S(2)}) async-start(), calls=%async_computation.23 | async-start | bytes 2359296 | tf_op jit(solution)/shard_map/all_gather | solution.py:103
  58.0 58.2 %copy-start.2 = (bf16[2,256,2048]{2,1,0:T(8,128)(2,1)S(1)}, bf16[2,256,2048]{2,1,0:T(8,128)(2,1)}, u32[]{:S(2)}) copy-start(bf16[2,256,2048]{2,1,0:T(8,128)(2,1)} %all-gather.12.cloned.1.call-done) | copy-start | bytes 6291460
  90.0 42.8 %copy-start.9 = (f32[2,256,512]{2,1,0:T(8,128)}, f32[2,256,512]{2,1,0:T(8,128)S(1)}, u32[]{:S(2)}) copy-start(f32[2,256,512]{2,1,0:T(8,128)S(1)} %get-tuple-element.91) | copy-start | bytes 3145732
  135.3 3.9 copy-start.11
  141.9 1.3 copy-start.26
  141.9 1.6 copy-start.27
  141.9 1.6 copy-start.28
  146.0 10.0 all-to-all-start.2
  156.0 10.1 all-to-all-start.1
  162.3 22.9 %copy-start.38 = (s32[2,1024]{1,0:T(2,128)S(1)}, s32[2,1024]{1,0:T(2,128)}, u32[]{:S(2)}) copy-start(s32[2,1024]{1,0:T(2,128)} %param.16) | copy-start | bytes 24580
  166.1 5.8 copy-start.31
  166.1 15.7 %all-to-all-start = ((bf16[2,256,4,128]{3,1,0,2:T(8,128)(2,1)}), bf16[2,256,4,128]{3,1,0,2:T(8,128)(2,1)}, u32[]{:S(2)}, u32[]{:S(2)}) async-start(bf16[2,256,4,128]{3,1,0,2:T(8,128)(2,1)} %bitcast.218), calls=%async_computation | async-start | bytes 1048576 | tf_op jit(solution)/shard_map/all_to_all | solution.py:141
  170.2 120.1 %reduce-scatter.12.cloned.1.call-start = ((), (), s32[]{:S(2)}) async-start(), calls=%async_computation.24 | async-start | bytes 5242880 | tf_op jit(solution)/shard_map/reduce_scatter | solution.py:77
  171.9 17.4 %copy-start.16 = (bf16[2,4,256,1,128]{4,2,1,0,3:T(8,128)(2,1)}, bf16[2,4,256,1,128]{4,2,1,0,3:T(8,128)(2,1)S(1)}, u32[]{:S(2)}) copy-start(bf16[2,4,256,1,128]{4,2,1,0,3:T(8,128)(2,1)S(1)} %copy.93) | copy-start | bytes 1572868
  185.3 5.2 copy-start.19
  189.3 3.3 copy-start
  194.1 19.8 %copy-start.14 = (bf16[2,128,1024]{2,1,0:T(8,128)(2,1)}, bf16[2,128,1024]{2,1,0:T(8,128)(2,1)S(1)}, u32[]{:S(2)}) copy-start(bf16[2,128,1024]{2,1,0:T(8,128)(2,1)S(1)} %convolution_convert_fusion.1) | copy-start | bytes 1572868
  213.9 77.8 %copy-start.18 = (bf16[2,64,2048]{2,1,0:T(8,128)(2,1)S(1)}, bf16[2,64,2048]{2,1,0:T(8,128)(2,1)}, u32[]{:S(2)}) copy-start(bf16[2,64,2048]{2,1,0:T(8,128)(2,1)} %param.15) | copy-start | bytes 1572868
  213.9 77.8 %copy-start.35 = (f32[2048]{0:T(1024)S(1)}, f32[2048]{0:T(1024)}, u32[]{:S(2)}) copy-start(f32[2048]{0:T(1024)} %param.27) | copy-start | bytes 24580
  214.0 133.1 %all-gather.24.cloned.1.call-start = ((), (), s32[]{:S(2)}) async-start(), calls=%async_computation.26 | async-start | bytes 9437184 | tf_op jit(solution)/shard_map/all_gather | solution.py:104
  214.7 180.1 %all-gather.22.cloned.1.call-start = ((), (), s32[]{:S(2)}) async-start(), calls=%async_computation.25 | async-start | bytes 2621440 | tf_op jit(solution)/shard_map/all_gather | solution.py:73
  294.0 155.8 %all-gather.26.cloned.1.call-start = ((), (), s32[]{:S(2)}) async-start(), calls=%async_computation.27 | async-start | bytes 9437184 | tf_op jit(solution)/shard_map/all_gather | solution.py:105
  294.7 211.1 %all-gather.28.cloned.1.call-start = ((), (), s32[]{:S(2)}) async-start(), calls=%async_computation.28 | async-start | bytes 9437184 | tf_op jit(solution)/shard_map/all_gather | solution.py:106
  295.3 298.0 %reduce-scatter.14.cloned.1.call-start = ((), (), s32[]{:S(2)}) async-start(), calls=%async_computation.29 | async-start | bytes 5242880 | tf_op jit(solution)/shard_map/reduce_scatter | solution.py:77
  516.4 78.4 %copy-start.4 = (bf16[2,64,2048]{2,1,0:T(8,128)(2,1)S(1)}, bf16[2,64,2048]{2,1,0:T(8,128)(2,1)}, u32[]{:S(2)}) copy-start(bf16[2,64,2048]{2,1,0:T(8,128)(2,1)} %param.29) | copy-start | bytes 1572868
  516.4 78.4 %copy-start.36 = (f32[2048]{0:T(1024)S(1)}, f32[2048]{0:T(1024)}, u32[]{:S(2)}) copy-start(f32[2048]{0:T(1024)} %param.28) | copy-start | bytes 24580
  516.4 128.6 %all-gather.30.cloned.1.call-start = ((), (), s32[]{:S(2)}) async-start(), calls=%async_computation.30 | async-start | bytes 2621440 | tf_op jit(solution)/shard_map/all_gather | solution.py:73
  598.7 152.0 %reduce-scatter.16.cloned.1.call-start = ((), (), s32[]{:S(2)}) async-start(), calls=%async_computation.31 | async-start | bytes 5242880 | tf_op jit(solution)/shard_map/reduce_scatter | solution.py:77
  656.9 8.5 copy-start.39
  656.9 8.5 copy-start.40
  674.9 77.8 %copy-start.3 = (f32[2,64,2048]{2,1,0:T(8,128)S(1)}, f32[2,64,2048]{2,1,0:T(8,128)}, u32[]{:S(2)}) copy-start(f32[2,64,2048]{2,1,0:T(8,128)} %reduce-scatter.14.cloned.1.call-done) | copy-start | bytes 3145732
  675.0 127.5 %all-gather.32.cloned.1.call-start = ((), (), s32[]{:S(2)}) async-start(), calls=%async_computation.32 | async-start | bytes 2621440 | tf_op jit(solution)/shard_map/all_gather | solution.py:73
  756.1 241.7 %reduce-scatter.24.cloned.1.call-start = ((), (), s32[]{:S(2)}) async-start(), calls=%async_computation.36 | async-start | bytes 4718592 | tf_op jit(solution)/shard_map/reduce_scatter | solution.py:294
  841.3 1.2 copy-start.15
  843.8 8.0 copy-start.17
  849.9 2.0 copy-start.1
  851.9 6.0 copy-start.29
  853.8 13.1 all-to-all-start.5
  866.9 14.5 all-to-all-start.6
  871.0 128.8 %reduce-scatter.22.cloned.1.call-start = ((), (), s32[]{:S(2)}) async-start(), calls=%async_computation.35 | async-start | bytes 4718592 | tf_op jit(solution)/shard_map/reduce_scatter | solution.py:293
  882.7 1.8 copy-start.12
  882.7 2.8 copy-start.10
  884.5 1.0 copy-start.6
  884.5 1.5 copy-start.7
  884.5 1.7 copy-start.8
  902.8 102.9 %reduce-scatter.20.cloned.1.call-start = ((), (), s32[]{:S(2)}) async-start(), calls=%async_computation.34 | async-start | bytes 4718592 | tf_op jit(solution)/shard_map/reduce_scatter | solution.py:292
  905.7 3.8 copy-start.21
  909.0 3.7 copy-start.23
  909.0 175.7 %reduce-scatter.18.cloned.1.call-start = ((), (), s32[]{:S(2)}) async-start(), calls=%async_computation.33 | async-start | bytes 5242880 | tf_op jit(solution)/shard_map/reduce_scatter | solution.py:77
  909.5 3.2 copy-start.30
  912.7 1.3 copy-start.25
  912.7 1.9 copy-start.34
  918.0 1.0 copy-start.33
  918.0 222.3 %reduce-scatter.26.cloned.1.call-start = ((), (), s32[]{:S(2)}) async-start(), calls=%async_computation.37 | async-start | bytes 4718592 | tf_op jit(solution)/shard_map/reduce_scatter | solution.py:295
  923.9 336.7 %reduce-scatter.32.cloned.1.call-start = ((), (), s32[]{:S(2)}) async-start(), calls=%async_computation.40 | async-start | bytes 18874368 | tf_op jit(solution)/shard_map/reduce_scatter | solution.py:298
  936.5 1.6 copy-start.37
  936.5 444.4 %reduce-scatter.28.cloned.1.call-start = ((), (), s32[]{:S(2)}) async-start(), calls=%async_computation.38 | async-start | bytes 18874368 | tf_op jit(solution)/shard_map/reduce_scatter | solution.py:296
  948.0 553.3 %reduce-scatter.30.cloned.1.call-start = ((), (), s32[]{:S(2)}) async-start(), calls=%async_computation.39 | async-start | bytes 18874368 | tf_op jit(solution)/shard_map/reduce_scatter | solution.py:297
  958.0 126.7 %copy-start.5 = (bf16[2,64,2048]{2,1,0:T(8,128)(2,1)S(1)}, bf16[2,64,2048]{2,1,0:T(8,128)(2,1)}, u32[]{:S(2)}) copy-start(bf16[2,64,2048]{2,1,0:T(8,128)(2,1)} %param.29) | copy-start | bytes 1572868
  958.0 126.7 %copy-start.13 = (f32[2,64,2048]{2,1,0:T(8,128)S(1)}, f32[2,64,2048]{2,1,0:T(8,128)}, u32[]{:S(2)}) copy-start(f32[2,64,2048]{2,1,0:T(8,128)} %reduce-scatter.16.cloned.1.call-done) | copy-start | bytes 3145732
  (4 other events, 3.2 us)
Sparse Core Ops, SparseCore 0:
  9.6 48.3 all-gather.11
  59.9 26.5 all-gather.15
  88.4 27.7 all-gather.17
  117.9 27.7 all-gather.13
  147.4 35.7 all-gather.19
  214.1 76.1 reduce-scatter.11
  292.2 54.7 all-gather.23
  349.1 45.6 all-gather.21
  396.7 53.0 all-gather.25
  451.6 54.2 all-gather.27
  516.5 76.7 reduce-scatter.13
  598.8 46.1 all-gather.29
  675.1 75.5 reduce-scatter.15
  756.2 46.1 all-gather.31
  841.4 54.3 reduce-scatter.23
  902.9 48.2 reduce-scatter.21
  954.5 51.2 reduce-scatter.19
  1007.9 76.7 reduce-scatter.17
  1088.6 51.6 reduce-scatter.25
  1144.3 116.1 reduce-scatter.31
  1264.7 116.1 reduce-scatter.27
  1385.1 116.1 reduce-scatter.29
where the time goes:
time: 1520 us; the launch traced here: 1510 us
  waiting for transfers between devices  1130 us (74%)
  matrix products  159 us (10%)
  blocking collectives  93.2 us (6%)
  local copies, waits for them, and re-layouts  49.8 us (3%)
  other arithmetic  35.7 us (2%)
  starting transfers between devices  21.8 us (1%)
    reduce_scatter x4, waiting for transfers between devices, sum_tokens(): return lax.psum_scatter(terms, 'tensor', scatter_dimension=1, tiled=True)  305 us
    all_gather x4, waiting for transfers between devices, gather_tokens(): return lax.all_gather(matrix_rows, 'tensor', axis=1, tiled=True)  184 us
    reduce_scatter x1, waiting for transfers between devices, body(): lax.psum_scatter(gate_wgrad, ('fsdp', 'ctx'), scatter_dimension=0, tiled=...  120 us
    reduce_scatter x1, waiting for transfers between devices, body(): lax.psum_scatter(up_wgrad, ('fsdp', 'ctx'), scatter_dimension=0, tiled=True)  120 us
    reduce_scatter x1, waiting for transfers between devices, body(): lax.psum_scatter(down_wgrad, ('fsdp', 'ctx'), scatter_dimension=0, tiled=...  120 us
    reduce_scatter x1, waiting for transfers between devices, body(): lax.psum_scatter(output_wgrad, ('fsdp', 'ctx'), scatter_dimension=0, tile...  53.2 us
    all_gather x1, waiting for transfers between devices, body(): lax.all_gather(gate_weight, ('fsdp', 'ctx'), axis=0, tiled=True)  51.1 us
    dot_general x7, matrix products, project(): jnp.einsum('xmj,je->xme', matrix_rows, weight_matrix, preferred_element_t...  48.6 us
  transfers between devices with their start and end apart: 27, of which 23 were waited for; matrix products, arithmetic and copies ran while one was open for 11% of the time, Pallas kernels for 0%

commit v1 on v0

--- a/solution.py
+++ b/solution.py
@@ -1,3 +1,4 @@
+import functools
 import jax
 import jax.numpy as jnp
 from jax import lax
@@ -8,6 +9,26 @@
 epsilon = 1e-06
 rope_theta = 500000.0
 masked_score = -1e30
+
+
+def types_connect(x_in, device_axis):
+    r1 = lax.psum(1, device_axis)
+    after = lax.axis_index(device_axis)
+    current_block, z, out_arr = (r1, after, x_in.shape[1])
+    inter, y2 = (x_in, 1)
+    while y2 < current_block:
+        log = []
+        dev_i = 0
+        while dev_i < current_block:
+            log.append((dev_i, (dev_i - y2) % current_block))
+            dev_i += 1
+        all_rows = lax.ppermute(inter, device_axis, log)
+        inter = jnp.concatenate([inter, all_rows], axis=1)
+        y2 = 2 * y2
+    return jnp.roll(inter, z * out_arr, axis=1)
+
+
+_enter_shelves = functools.partial(types_connect, device_axis="tensor")
 
 
 def rope_tables(position_ids):
@@ -70,7 +91,7 @@
 
 
 def gather_tokens(matrix_rows):
-    return lax.all_gather(matrix_rows, "tensor", axis=1, tiled=True)
+    return _enter_shelves(matrix_rows)
 
 
 def sum_tokens(terms):

time: 1520 us -> 1510 us (level)
  starting transfers between devices: 21.8 us -> 46.7 us
  local copies, waits for them, and re-layouts: 49.8 us -> 32.5 us
  other arithmetic: 35.7 us -> 51 us
    ppermute x0 -> x8, waiting for transfers between devices: none -> 222 us  [types_connect(): all_rows = lax.ppermute(inter, device_axis, log)]
    all_gather x4 -> x0, waiting for transfers between devices: 184 us -> none  [gather_tokens(): return lax.all_gather(matrix_rows, 'tensor', axis=1, tiled=True)]
    reduce_scatter x4, waiting for transfers between devices: 305 us -> 226 us  [sum_tokens(): return lax.psum_scatter(terms, 'tensor', scatter_dimension=1, tiled=True)]
    reduce_scatter x1, waiting for transfers between devices: 0.01 us -> 55.1 us  [body(): lax.psum_scatter(value_wgrad, ('fsdp', 'ctx'), scatter_dimension=0, tiled...]
    reduce_scatter x1, waiting for transfers between devices: 0.01 us -> 55 us  [body(): lax.psum_scatter(key_wgrad, ('fsdp', 'ctx'), scatter_dimension=0, tiled=T...]
    reduce_scatter x1, waiting for transfers between devices: 3.87 us -> 55 us  [body(): lax.psum_scatter(query_wgrad, ('fsdp', 'ctx'), scatter_dimension=0, tiled...]
    all_gather x1, waiting for transfers between devices: 51.1 us -> 0.02 us  [body(): lax.all_gather(gate_weight, ('fsdp', 'ctx'), axis=0, tiled=True)]
    all_gather x1, waiting for transfers between devices: 28.5 us -> 0.02 us  [body(): lax.all_gather(query_weight, ('fsdp', 'ctx'), axis=0, tiled=True)]
  transfers between devices with their start and end apart: 27 -> 32, of which waited for: 23 -> 25; matrix products, arithmetic and copies ran while one was open for 11% -> 9% of each run, Pallas kernels for 0% -> 0%
where the time goes in v1:
time: 1510 us; the launch traced here: 1500 us
  waiting for transfers between devices  1120 us (74%)
  matrix products  146 us (10%)
  blocking collectives  85.9 us (6%)
  other arithmetic  51 us (3%)
  starting transfers between devices  46.7 us (3%)
  local copies, waits for them, and re-layouts  32.5 us (2%)
  between operations  15.5 us (1%)
    reduce_scatter x4, waiting for transfers between devices, sum_tokens(): return lax.psum_scatter(terms, 'tensor', scatter_dimension=1, tiled=True)  226 us
    ppermute x8, waiting for transfers between devices, types_connect(): all_rows = lax.ppermute(inter, device_axis, log)  222 us
    reduce_scatter x1, waiting for transfers between devices, body(): lax.psum_scatter(up_wgrad, ('fsdp', 'ctx'), scatter_dimension=0, tiled=True)  120 us
    reduce_scatter x1, waiting for transfers between devices, body(): lax.psum_scatter(down_wgrad, ('fsdp', 'ctx'), scatter_dimension=0, tiled=...  120 us
    reduce_scatter x1, waiting for transfers between devices, body(): lax.psum_scatter(gate_wgrad, ('fsdp', 'ctx'), scatter_dimension=0, tiled=...  120 us
    reduce_scatter x1, waiting for transfers between devices, body(): lax.psum_scatter(value_wgrad, ('fsdp', 'ctx'), scatter_dimension=0, tiled...  55.1 us
    reduce_scatter x1, waiting for transfers between devices, body(): lax.psum_scatter(key_wgrad, ('fsdp', 'ctx'), scatter_dimension=0, tiled=T...  55 us
    reduce_scatter x1, waiting for transfers between devices, body(): lax.psum_scatter(query_wgrad, ('fsdp', 'ctx'), scatter_dimension=0, tiled...  55 us
  transfers between devices with their start and end apart: 32, of which 25 were waited for; matrix products, arithmetic and copies ran while one was open for 9% of the time, Pallas kernels for 0%

profile of v1, /device:TPU:0, one launch (start us, length us, event | category | flops | bytes accessed | tf_op | source)
XLA Modules:
  0.0 1499.1 jit_solution(5970796328032420266)
XLA Ops:
  9.4 5.1 collective-permute-start
  14.6 11.5 collective-permute-done
  32.6 42.2 %collective-permute-done.1 = bf16[2,128,2048]{2,1,0:T(8,128)(2,1)} collective-permute-done((bf16[2,128,2048]{2,1,0:T(8,128)(2,1)S(1)}, bf16[2,128,2048]{2,1,0:T(8,128)(2,1)}, u32[]{:S(2)}, u32[]{:S(2)}) %collective-permute-start.1) | collective-permute-done | bytes 1048608 | tf_op jit(solution)/shard_map/ppermute | solution.py:25
  74.8 4.9 fusion.34
  79.8 3.7 multiply_reduce_fusion.8
  83.5 3.9 multiply_reduce_fusion.7
  87.4 10.8 all-reduce.2
  107.2 3.7 all-to-all-start.2
  113.1 6.8 all-to-all-done.2
  119.9 3.5 all-to-all-start.1
  127.2 8.6 all-to-all-done.1
  135.7 3.5 all-to-all-start
  141.1 6.0 all-to-all-done
  147.8 3.8 fusion.84
  156.9 10.0 all_to_all.108
  167.6 5.1 fusion.39
  174.9 71.5 %reduce-scatter.12.cloned.1.call-done = f32[2,64,2048]{2,1,0:T(8,128)} async-done(((f32[2,256,2048]{2,1,0:T(8,128)}), f32[2,64,2048]{2,1,0:T(8,128)}) %reduce-scatter.12.cloned.1.call-update) | async-done | bytes 1048592 | tf_op jit(solution)/shard_map/reduce_scatter | solution.py:98
  249.2 2.8 collective-permute-start.2
  252.1 11.3 collective-permute-done.2
  266.1 44.9 %collective-permute-done.3 = bf16[2,128,2048]{2,1,0:T(8,128)(2,1)S(1)} collective-permute-done((bf16[2,128,2048]{2,1,0:T(8,128)(2,1)S(1)}, bf16[2,128,2048]{2,1,0:T(8,128)(2,1)S(1)}, u32[]{:S(2)}, u32[]{:S(2)}) %collective-permute-start.3) | collective-permute-done | bytes 1048608 | tf_op jit(solution)/shard_map/ppermute | solution.py:25
  311.1 4.9 fusion.29
  316.1 10.1 fusion.10
  326.2 33.0 %all-gather.18.cloned.1.call-done = bf16[2048,2048]{1,0:T(8,128)(2,1)} async-done(((bf16[256,2048]{1,0:T(8,128)(2,1)}), bf16[2048,2048]{1,0:T(8,128)(2,1)}) %all-gather.18.cloned.1.call-update) | async-done | bytes 8388624 | tf_op jit(solution)/shard_map/all_gather | solution.py:126
  359.1 10.8 multiply_convert_fusion.3
  369.9 45.4 %all-gather.20.cloned.1.call-done = bf16[2048,2048]{1,0:T(8,128)(2,1)} async-done(((bf16[256,2048]{1,0:T(8,128)(2,1)}), bf16[2048,2048]{1,0:T(8,128)(2,1)}) %all-gather.20.cloned.1.call-update) | async-done | bytes 8388624 | tf_op jit(solution)/shard_map/all_gather | solution.py:127
  415.3 10.6 fusion.2
  425.9 76.9 %reduce-scatter.14.cloned.1.call-done = f32[2,64,2048]{2,1,0:T(8,128)} async-done(((f32[2,256,2048]{2,1,0:T(8,128)}), f32[2,64,2048]{2,1,0:T(8,128)}) %reduce-scatter.14.cloned.1.call-update) | async-done | bytes 1048592 | tf_op jit(solution)/shard_map/reduce_scatter | solution.py:98
  507.5 2.9 collective-permute-start.4
  510.4 11.3 collective-permute-done.4
  524.4 45.0 %collective-permute-done.5 = bf16[2,128,2048]{2,1,0:T(8,128)(2,1)S(1)} collective-permute-done((bf16[2,128,2048]{2,1,0:T(8,128)(2,1)S(1)}, bf16[2,128,2048]{2,1,0:T(8,128)(2,1)S(1)}, u32[]{:S(2)}, u32[]{:S(2)}) %collective-permute-start.5) | collective-permute-done | bytes 1048608 | tf_op jit(solution)/shard_map/ppermute | solution.py:25
  569.4 5.0 fusion.24
  574.4 11.4 multiply_convert_fusion.2
  585.9 6.2 fusion.4
  592.1 8.4 fusion.14
  600.5 77.8 %reduce-scatter.16.cloned.1.call-done = f32[2,64,2048]{2,1,0:T(8,128)} async-done(((f32[2,256,2048]{2,1,0:T(8,128)}), f32[2,64,2048]{2,1,0:T(8,128)}) %reduce-scatter.16.cloned.1.call-update) | async-done | bytes 1048592 | tf_op jit(solution)/shard_map/reduce_scatter | solution.py:98
  682.6 3.0 collective-permute-start.6
  685.5 11.3 collective-permute-done.6
  699.6 44.9 %collective-permute-done.7 = bf16[2,128,2048]{2,1,0:T(8,128)(2,1)S(1)} collective-permute-done((bf16[2,128,2048]{2,1,0:T(8,128)(2,1)S(1)}, bf16[2,128,2048]{2,1,0:T(8,128)(2,1)S(1)}, u32[]{:S(2)}, u32[]{:S(2)}) %collective-permute-start.7) | collective-permute-done | bytes 1048608 | tf_op jit(solution)/shard_map/ppermute | solution.py:25
  744.6 4.9 fusion.19
  750.9 10.5 all_to_all.109
  764.0 5.2 multiply_convert_fusion
  773.2 3.5 all-to-all-start.5
  776.7 3.7 fusion.62
  783.3 3.5 all-to-all-start.6
  786.7 4.9 fusion.70
  794.0 4.2 all-to-all-start.7
  798.6 6.2 all-to-all-done.7
  812.2 13.8 all-reduce.1
  832.6 3.3 add_add_fusion
  836.9 4.9 convolution_bitcast_fusion.3
  842.9 3.3 convolution_bitcast_fusion.4
  846.2 4.4 convolution_bitcast_fusion.5
  850.7 3.3 convolution_bitcast_fusion.6
  855.6 9.8 convolution_bitcast_fusion
  867.0 9.8 convolution_bitcast_fusion.2
  876.9 9.9 convolution_bitcast_fusion.1
  887.3 40.7 %all-reduce = (f32[2048]{0:T(1024)}, f32[2048]{0:T(1024)}, f32[2048]{0:T(1024)}, f32[2048]{0:T(1024)}) all-reduce(f32[2048]{0:T(1024)S(1)} %dynamic_update_slice.6, f32[2048]{0:T(1024)S(1)} %dynamic_update_slice.7, f32[2048]{0:T(1024)S(1)} %get-tuple-element.14, ...), channel_id=1, replica_groups=mesh['fsdp'=2,'ctx'=4,'tensor'=4] {'fsdp','ctx','tensor'}, use_global_device_ids=true, to_apply=%region_26.28 | all-reduce | flops 8192 | bytes 65536 | tf_op jit(solution)/shard_map/psum | solution.py:301
  930.5 35.8 %reduce-scatter.26.cloned.1.call-done = f32[256,512]{1,0:T(8,128)} async-done(((f32[2048,512]{1,0:T(8,128)}), f32[256,512]{1,0:T(8,128)}) %reduce-scatter.26.cloned.1.call-update) | async-done | bytes 524304 | tf_op jit(solution)/shard_map/reduce_scatter | solution.py:316
  966.2 55.1 %reduce-scatter.24.cloned.1.call-done = f32[256,512]{1,0:T(8,128)} async-done(((f32[2048,512]{1,0:T(8,128)}), f32[256,512]{1,0:T(8,128)}) %reduce-scatter.24.cloned.1.call-update) | async-done | bytes 524304 | tf_op jit(solution)/shard_map/reduce_scatter | solution.py:315
  1021.4 55.0 %reduce-scatter.22.cloned.1.call-done = f32[256,512]{1,0:T(8,128)} async-done(((f32[2048,512]{1,0:T(8,128)}), f32[256,512]{1,0:T(8,128)}) %reduce-scatter.22.cloned.1.call-update) | async-done | bytes 524304 | tf_op jit(solution)/shard_map/reduce_scatter | solution.py:314
  1076.3 55.0 %reduce-scatter.20.cloned.1.call-done = f32[256,512]{1,0:T(8,128)} async-done(((f32[2048,512]{1,0:T(8,128)}), f32[256,512]{1,0:T(8,128)}) %reduce-scatter.20.cloned.1.call-update) | async-done | bytes 524304 | tf_op jit(solution)/shard_map/reduce_scatter | solution.py:313
  1131.3 120.2 %reduce-scatter.32.cloned.1.call-done = f32[256,2048]{1,0:T(8,128)} async-done(((f32[2048,2048]{1,0:T(8,128)}), f32[256,2048]{1,0:T(8,128)}) %reduce-scatter.32.cloned.1.call-update) | async-done | bytes 2097168 | tf_op jit(solution)/shard_map/reduce_scatter | solution.py:319
  1251.5 120.2 %reduce-scatter.28.cloned.1.call-done = f32[256,2048]{1,0:T(8,128)} async-done(((f32[2048,2048]{1,0:T(8,128)}), f32[256,2048]{1,0:T(8,128)}) %reduce-scatter.28.cloned.1.call-update) | async-done | bytes 2097168 | tf_op jit(solution)/shard_map/reduce_scatter | solution.py:317
  1371.8 120.2 %reduce-scatter.30.cloned.1.call-done = f32[256,2048]{1,0:T(8,128)} async-done(((f32[2048,2048]{1,0:T(8,128)}), f32[256,2048]{1,0:T(8,128)}) %reduce-scatter.30.cloned.1.call-update) | async-done | bytes 2097168 | tf_op jit(solution)/shard_map/reduce_scatter | solution.py:318
  (242 shorter events, 89.8 us)
Async XLA Ops:
  7.2 72.6 %all-gather.10.cloned.1.call-start = ((), (), s32[]{:S(2)}) async-start(), calls=%async_computation.20 | async-start | bytes 2359296 | tf_op jit(solution)/shard_map/all_gather | solution.py:121
  7.9 75.5 %all-gather.12.cloned.1.call-start = ((), (), s32[]{:S(2)}) async-start(), calls=%async_computation.21 | async-start | bytes 2359296 | tf_op jit(solution)/shard_map/all_gather | solution.py:122
  8.7 114.8 %all-gather.8.cloned.1.call-start = ((), (), s32[]{:S(2)}) async-start(), calls=%async_computation.19 | async-start | bytes 2359296 | tf_op jit(solution)/shard_map/all_gather | solution.py:123
  9.4 158.2 %all-gather.14.cloned.1.call-start = ((), (), s32[]{:S(2)}) async-start(), calls=%async_computation.22 | async-start | bytes 2359296 | tf_op jit(solution)/shard_map/all_gather | solution.py:124
  9.4 16.6 %collective-permute-start = (bf16[2,64,2048]{2,1,0:T(8,128)(2,1)}, bf16[2,64,2048]{2,1,0:T(8,128)(2,1)S(1)}, u32[]{:S(2)}, u32[]{:S(2)}) collective-permute-start(bf16[2,64,2048]{2,1,0:T(8,128)(2,1)} %param.17), channel_id=1, source_target_pairs={{0,3},{1,0},{2,1},{3,2},{4,7},{5,4},{6,5},{7,6},{8,11},{9,8},{10,9... | collective-permute-start | bytes 1572872 | tf_op jit(solution)/shard_map/ppermute | solution.py:25
  27.2 47.6 %collective-permute-start.1 = (bf16[2,128,2048]{2,1,0:T(8,128)(2,1)S(1)}, bf16[2,128,2048]{2,1,0:T(8,128)(2,1)}, u32[]{:S(2)}, u32[]{:S(2)}) collective-permute-start(bf16[2,128,2048]{2,1,0:T(8,128)(2,1)S(1)} %pad_maximum_fusion), channel_id=1, source_target_pairs={{0,2},{1,3},{2,0},{3,1},{4,6},{5,7},{6,4},{7,5},{8,10},{9,11},{10,... | collective-permute-start | bytes 3145736 | tf_op jit(solution)/shard_map/ppermute | solution.py:25
  83.4 15.9 %copy-start.11 = (f32[2,256,512]{2,1,0:T(8,128)}, f32[2,256,512]{2,1,0:T(8,128)S(1)}, u32[]{:S(2)}) copy-start(f32[2,256,512]{2,1,0:T(8,128)S(1)} %get-tuple-element.53) | copy-start | bytes 3145732
  87.4 15.5 %copy-start.14 = (f32[2,256,512]{2,1,0:T(8,128)}, f32[2,256,512]{2,1,0:T(8,128)S(1)}, u32[]{:S(2)}) copy-start(f32[2,256,512]{2,1,0:T(8,128)S(1)} %get-tuple-element.55) | copy-start | bytes 3145732
  106.1 17.4 %copy-start.33 = (bf16[2,256,2048]{2,1,0:T(8,128)(2,1)S(1)}, bf16[2,256,2048]{2,1,0:T(8,128)(2,1)}, u32[]{:S(2)}) copy-start(bf16[2,256,2048]{2,1,0:T(8,128)(2,1)} %copy-done.32) | copy-start | bytes 6291460
  107.2 12.7 all-to-all-start.2
  119.9 15.9 %all-to-all-start.1 = ((bf16[2,256,4,128]{3,1,0,2:T(8,128)(2,1)}), bf16[2,256,4,128]{3,1,0,2:T(8,128)(2,1)S(1)}, u32[]{:S(2)}, u32[]{:S(2)}) async-start(bf16[2,256,4,128]{3,1,0,2:T(8,128)(2,1)} %copy.90), calls=%async_computation.1 | async-start | bytes 1048576 | tf_op jit(solution)/shard_map/all_to_all | solution.py:160
  126.3 21.5 %copy-start.52 = (s32[2,1024]{1,0:T(2,128)S(1)}, s32[2,1024]{1,0:T(2,128)}, u32[]{:S(2)}) copy-start(s32[2,1024]{1,0:T(2,128)} %param.18) | copy-start | bytes 24580
  135.7 11.4 all-to-all-start
  139.2 107.2 %reduce-scatter.12.cloned.1.call-start = ((), (), s32[]{:S(2)}) async-start(), calls=%async_computation.23 | async-start | bytes 5242880 | tf_op jit(solution)/shard_map/reduce_scatter | solution.py:98
  141.1 10.6 copy-start.20
  141.1 10.5 copy-start.28
  156.5 16.2 %copy-start.18 = (bf16[2,128,1024]{2,1,0:T(8,128)(2,1)}, bf16[2,128,1024]{2,1,0:T(8,128)(2,1)S(1)}, u32[]{:S(2)}) copy-start(bf16[2,128,1024]{2,1,0:T(8,128)(2,1)S(1)} %convolution_convert_fusion.1) | copy-start | bytes 1572868
  172.7 75.0 %copy-start.17 = (bf16[2,64,2048]{2,1,0:T(8,128)(2,1)S(1)}, bf16[2,64,2048]{2,1,0:T(8,128)(2,1)}, u32[]{:S(2)}) copy-start(bf16[2,64,2048]{2,1,0:T(8,128)(2,1)} %param.17) | copy-start | bytes 1572868
  172.7 75.0 %copy-start.50 = (f32[2048]{0:T(1024)S(1)}, f32[2048]{0:T(1024)}, u32[]{:S(2)}) copy-start(f32[2048]{0:T(1024)} %param.29) | copy-start | bytes 24580
  172.8 143.3 %all-gather.16.cloned.1.call-start = ((), (), s32[]{:S(2)}) async-start(), calls=%async_computation.24 | async-start | bytes 9437184 | tf_op jit(solution)/shard_map/all_gather | solution.py:125
  173.3 185.8 %all-gather.18.cloned.1.call-start = ((), (), s32[]{:S(2)}) async-start(), calls=%async_computation.25 | async-start | bytes 9437184 | tf_op jit(solution)/shard_map/all_gather | solution.py:126
  174.1 241.2 %all-gather.20.cloned.1.call-start = ((), (), s32[]{:S(2)}) async-start(), calls=%async_computation.26 | async-start | bytes 9437184 | tf_op jit(solution)/shard_map/all_gather | solution.py:127
  174.8 328.0 %reduce-scatter.14.cloned.1.call-start = ((), (), s32[]{:S(2)}) async-start(), calls=%async_computation.27 | async-start | bytes 5242880 | tf_op jit(solution)/shard_map/reduce_scatter | solution.py:98
  249.2 14.2 collective-permute-start.2
  263.5 47.6 %collective-permute-start.3 = (bf16[2,128,2048]{2,1,0:T(8,128)(2,1)S(1)}, bf16[2,128,2048]{2,1,0:T(8,128)(2,1)S(1)}, u32[]{:S(2)}, u32[]{:S(2)}) collective-permute-start(bf16[2,128,2048]{2,1,0:T(8,128)(2,1)S(1)} %pad_maximum_fusion.1), channel_id=1, source_target_pairs={{0,2},{1,3},{2,0},{3,1},{4,6},{5,7},{6,4},{7,5},{8,10},{9,11},{10,... | collective-permute-start | bytes 3145736 | tf_op jit(solution)/shard_map/ppermute | solution.py:25
  316.0 43.1 %copy-start.36 = (bf16[2,256,2048]{2,1,0:T(8,128)(2,1)}, bf16[2,256,2048]{2,1,0:T(8,128)(2,1)S(1)}, u32[]{:S(2)}) copy-start(bf16[2,256,2048]{2,1,0:T(8,128)(2,1)S(1)} %fusion.29) | copy-start | bytes 6291460
  425.9 78.3 %copy-start.4 = (bf16[2,64,2048]{2,1,0:T(8,128)(2,1)S(1)}, bf16[2,64,2048]{2,1,0:T(8,128)(2,1)}, u32[]{:S(2)}) copy-start(bf16[2,64,2048]{2,1,0:T(8,128)(2,1)} %param.31) | copy-start | bytes 1572868
  425.9 78.3 %copy-start.51 = (f32[2048]{0:T(1024)S(1)}, f32[2048]{0:T(1024)}, u32[]{:S(2)}) copy-start(f32[2048]{0:T(1024)} %param.30) | copy-start | bytes 24580
  425.9 252.5 %reduce-scatter.16.cloned.1.call-start = ((), (), s32[]{:S(2)}) async-start(), calls=%async_computation.28 | async-start | bytes 5242880 | tf_op jit(solution)/shard_map/reduce_scatter | solution.py:98
  505.9 68.5 %copy-start.54 = (f32[2,256,2048]{2,1,0:T(8,128)S(1)}, f32[2,256,2048]{2,1,0:T(8,128)}, u32[]{:S(2)}) copy-start(f32[2,256,2048]{2,1,0:T(8,128)} %fusion.10) | copy-start | bytes 12582916
  507.5 14.2 collective-permute-start.4
  521.8 47.6 %collective-permute-start.5 = (bf16[2,128,2048]{2,1,0:T(8,128)(2,1)S(1)}, bf16[2,128,2048]{2,1,0:T(8,128)(2,1)S(1)}, u32[]{:S(2)}, u32[]{:S(2)}) collective-permute-start(bf16[2,128,2048]{2,1,0:T(8,128)(2,1)S(1)} %pad_maximum_fusion.2), channel_id=1, source_target_pairs={{0,2},{1,3},{2,0},{3,1},{4,6},{5,7},{6,4},{7,5},{8,10},{9,11},{10,... | collective-permute-start | bytes 3145736 | tf_op jit(solution)/shard_map/ppermute | solution.py:25
  569.4 16.4 %slice-start.2 = ((s8[8388608]{0:T(1024)(128)(4,1)}), s8[4194304]{0:T(1024)(128)(4,1)S(1)}, s32[]{:S(2)}) async-start(s8[8388608]{0:T(1024)(128)(4,1)} %bitcast.220), calls=%async_computation.39 | async-start | bytes 8388608
  569.4 22.7 %slice-start = ((s8[8388608]{0:T(1024)(128)(4,1)}), s8[4194304]{0:T(1024)(128)(4,1)S(1)}, s32[]{:S(2)}) async-start(s8[8388608]{0:T(1024)(128)(4,1)} %bitcast.218), calls=%async_computation.37 | async-start | bytes 8388608
  574.4 11.5 copy-start.38
  574.4 11.5 slice-start.3
  574.4 17.7 %slice-start.1 = ((s8[8388608]{0:T(1024)(128)(4,1)}), s8[4194304]{0:T(1024)(128)(4,1)S(1)}, s32[]{:S(2)}) async-start(s8[8388608]{0:T(1024)(128)(4,1)} %bitcast.218), calls=%async_computation.38 | async-start | bytes 8388608
  585.8 6.2 copy-start.53
  600.5 77.9 %copy-start.3 = (f32[2,64,2048]{2,1,0:T(8,128)S(1)}, f32[2,64,2048]{2,1,0:T(8,128)}, u32[]{:S(2)}) copy-start(f32[2,64,2048]{2,1,0:T(8,128)} %reduce-scatter.12.cloned.1.call-done) | copy-start | bytes 3145732
  600.5 79.5 %copy-start.2 = (f32[2,64,2048]{2,1,0:T(8,128)S(1)}, f32[2,64,2048]{2,1,0:T(8,128)}, u32[]{:S(2)}) copy-start(f32[2,64,2048]{2,1,0:T(8,128)} %reduce-scatter.14.cloned.1.call-done) | copy-start | bytes 3145732
  682.6 66.9 %copy-start.35 = (bf16[2048,512]{1,0:T(8,128)(2,1)S(1)}, bf16[2048,512]{1,0:T(8,128)(2,1)}, u32[]{:S(2)}) copy-start(bf16[2048,512]{1,0:T(8,128)(2,1)} %all-gather.14.cloned.1.call-done) | copy-start | bytes 6291460
  682.6 14.3 collective-permute-start.6
  697.0 47.6 %collective-permute-start.7 = (bf16[2,128,2048]{2,1,0:T(8,128)(2,1)S(1)}, bf16[2,128,2048]{2,1,0:T(8,128)(2,1)S(1)}, u32[]{:S(2)}, u32[]{:S(2)}) collective-permute-start(bf16[2,128,2048]{2,1,0:T(8,128)(2,1)S(1)} %pad_maximum_fusion.3), channel_id=1, source_target_pairs={{0,2},{1,3},{2,0},{3,1},{4,6},{5,7},{6,4},{7,5},{8,10},{9,11},{10,... | collective-permute-start | bytes 3145736 | tf_op jit(solution)/shard_map/ppermute | solution.py:25
  750.8 11.9 copy-start.19
  750.8 13.2 copy-start.23
  764.0 7.3 copy-start.21
  771.3 5.4 copy-start.29
  773.2 10.0 all-to-all-start.5
  783.3 8.4 copy-start.41
  783.3 10.7 all-to-all-start.6
  792.8 16.3 %copy-start.27 = (f32[2,256,64]{2,1,0:T(8,128)S(1)}, f32[2,256,64]{2,1,0:T(8,128)}, u32[]{:S(2)}) copy-start(f32[2,256,64]{2,1,0:T(8,128)} %get-tuple-element.51) | copy-start | bytes 393220
  794.0 10.9 all-to-all-start.7
  798.1 129.9 %reduce-scatter.18.cloned.1.call-start = ((), (), s32[]{:S(2)}) async-start(), calls=%async_computation.29 | async-start | bytes 5242880 | tf_op jit(solution)/shard_map/reduce_scatter | solution.py:98
  811.7 16.8 %copy-start.6 = (f32[2,256,4,64]{3,1,2,0:T(8,128)S(1)}, f32[2,256,4,64]{3,1,2,0:T(8,128)}, u32[]{:S(2)}) copy-start(f32[2,256,4,64]{3,1,2,0:T(8,128)} %copy-done.5) | copy-start | bytes 1572868
  812.2 16.4 %copy-start.8 = (f32[2,256,4,64]{3,1,2,0:T(8,128)S(1)}, f32[2,256,4,64]{3,1,2,0:T(8,128)}, u32[]{:S(2)}) copy-start(f32[2,256,4,64]{3,1,2,0:T(8,128)} %copy-done.7) | copy-start | bytes 1572868
  835.9 6.0 copy-start.34
  835.9 130.3 %reduce-scatter.26.cloned.1.call-start = ((), (), s32[]{:S(2)}) async-start(), calls=%async_computation.33 | async-start | bytes 4718592 | tf_op jit(solution)/shard_map/reduce_scatter | solution.py:316
  841.8 179.5 %reduce-scatter.24.cloned.1.call-start = ((), (), s32[]{:S(2)}) async-start(), calls=%async_computation.32 | async-start | bytes 4718592 | tf_op jit(solution)/shard_map/reduce_scatter | solution.py:315
  846.2 230.2 %reduce-scatter.22.cloned.1.call-start = ((), (), s32[]{:S(2)}) async-start(), calls=%async_computation.31 | async-start | bytes 4718592 | tf_op jit(solution)/shard_map/reduce_scatter | solution.py:314
  850.6 280.7 %reduce-scatter.20.cloned.1.call-start = ((), (), s32[]{:S(2)}) async-start(), calls=%async_computation.30 | async-start | bytes 4718592 | tf_op jit(solution)/shard_map/reduce_scatter | solution.py:313
  854.0 397.5 %reduce-scatter.32.cloned.1.call-start = ((), (), s32[]{:S(2)}) async-start(), calls=%async_computation.36 | async-start | bytes 18874368 | tf_op jit(solution)/shard_map/reduce_scatter | solution.py:319
  865.4 506.3 %reduce-scatter.28.cloned.1.call-start = ((), (), s32[]{:S(2)}) async-start(), calls=%async_computation.34 | async-start | bytes 18874368 | tf_op jit(solution)/shard_map/reduce_scatter | solution.py:317
  876.8 615.2 %reduce-scatter.30.cloned.1.call-start = ((), (), s32[]{:S(2)}) async-start(), calls=%async_computation.35 | async-start | bytes 18874368 | tf_op jit(solution)/shard_map/reduce_scatter | solution.py:318
  886.8 41.3 %copy-start.16 = (f32[2,64,2048]{2,1,0:T(8,128)S(1)}, f32[2,64,2048]{2,1,0:T(8,128)}, u32[]{:S(2)}) copy-start(f32[2,64,2048]{2,1,0:T(8,128)} %reduce-scatter.16.cloned.1.call-done) | copy-start | bytes 3145732
  (27 other events, 57.7 us)
Sparse Core Ops, SparseCore 0:
  9.9 30.4 all-gather.9
  42.3 27.7 all-gather.11
  72.0 27.7 all-gather.7
  101.5 35.7 all-gather.13
  172.9 73.4 reduce-scatter.11
  248.1 54.7 all-gather.15
  304.8 54.2 all-gather.17
  361.0 54.2 all-gather.19
  426.0 76.7 reduce-scatter.13
  600.7 77.6 reduce-scatter.15
  836.1 74.4 reduce-scatter.17
  914.4 51.8 reduce-scatter.25
  970.2 51.1 reduce-scatter.23
  1025.1 51.1 reduce-scatter.21
  1080.1 51.1 reduce-scatter.19
  1135.3 116.1 reduce-scatter.31
  1255.5 116.1 reduce-scatter.27
  1375.8 116.2 reduce-scatter.29
